TPU v7x, 32 devices: a whole 2x2x4 slice. The times are simulated.
32 devices in a mesh: pair: 2 (over x), seq: 8 (over z, y), head: 2 (over core).
Axes of the slice: x: 2, y: 2, z: 4, core: 2. Of those that a mesh axis runs over, the one named last changes fastest.
Arguments:
- queries: bfloat16 [2, 512, 2, 3584], P('pair', 'seq', None, 'head'), may hold values from -6 to 6
- answer_keys: bfloat16 [2, 512, 2, 512], P('pair', 'seq', None, 'head'), may hold values from -6 to 6
- answer_values: bfloat16 [2, 512, 2, 512], P('pair', 'seq', None, 'head'), may hold values from -6 to 6
- prefix_keys: bfloat16 [768, 512], P(('pair', 'seq'), 'head'), may hold values from -8 to 8
- prefix_values: bfloat16 [768, 512], P(('pair', 'seq'), 'head'), may hold values from -6 to 6
- grad_out: bfloat16 [2, 512, 2, 3584], P('pair', 'seq', None, 'head'), may hold values from -6 to 6
- answer_length: int32 [2, 2], P('pair'), may hold values from 128 to 512
- prefix_limit: int32 [2, 2], P('pair'), may hold values from 384 to 768
Outputs:
- attention_out: bfloat16 [2, 512, 2, 3584], P('pair', 'seq', None, 'head')
- grad_queries: bfloat16 [2, 512, 2, 3584], P('pair', 'seq', None, 'head')
- grad_answer_keys: bfloat16 [2, 512, 2, 512], P('pair', 'seq', None, 'head')
- grad_answer_values: bfloat16 [2, 512, 2, 512], P('pair', 'seq', None, 'head')
- grad_prefix_keys: float32 [768, 512], P(('pair', 'seq'), 'head')
- grad_prefix_values: float32 [768, 512], P(('pair', 'seq'), 'head')
All inputs are finite; a program needn't handle non-finite values.
Results may differ from a plain program's by a relative error of at most 0.015.
Values may be sent and summed in bfloat16 or wider, within the bound.
A program may use at most 64 MiB of HBM per device.

v0:
```python
import functools
import math

import jax
import jax.numpy as jnp
from jax import lax
from jax.experimental import pallas as pl
from jax.experimental.pallas import tpu as pltpu
from jax.sharding import PartitionSpec as P

HEAD_DIM = 128
FILL = -1e30
VM = pltpu.VMEM


def split_seq(seq_size):
    inner = 2 if seq_size % 2 == 0 else 1
    return seq_size // inner, inner


def place(pair_size, seq_size):
    outer, inner = split_seq(seq_size)
    p = lax.axis_index("pair")
    s = lax.axis_index("seq")
    z, y = s // inner, s % inner
    return outer, inner, p, s, z, y


def greet(pair_size, outer, inner, p, z, y):
    barrier = pltpu.get_barrier_semaphore()
    for j in range(1, pair_size):
        pl.semaphore_signal(barrier, inc=1, device_id={"pair": (p + j) % pair_size})
    for j in range(1, inner):
        pl.semaphore_signal(barrier, inc=1, device_id={"seq": z * inner + (y + j) % inner})
    for k in range(1, outer):
        pl.semaphore_signal(barrier, inc=1, device_id={"seq": ((z + k) % outer) * inner + y})
    pl.semaphore_wait(barrier, pair_size + inner + outer - 3)


def chunks_of(slots, most):
    size = math.gcd(slots, most)
    return [(low, low + size) for low in range(0, slots, size)]


def flat_rows(block):
    return block.reshape(block.shape[0] * block.shape[1], block.shape[2])


def layer_kernel(
    pair_size, seq_size, batch, kv_heads, group,
    limits, lengths, q_ref, d_ref, ak_in, av_in, pk_in, pv_in,
    out_ref, dq_ref, ak_ref, av_ref, pk_ref, pv_ref,
    a_in, p_in, a_g, p_g, at_ref, pt_ref, e_ref, low_ref, acc_ref,
    rx, ry_p, rz_p, ry_a, rz_a, sy_p, sz_p, sz_a, own_a, own_p,
    gaz_s, gaz_r, gpz_s, gpz_r, gay_s, gay_r, gpy_s, gpy_r, gpx_s, gpx_r,
    saz_s, saz_r, spz_s, spz_r, say_s, say_r, spy_s, spy_r, spx_s, spx_r,
):
    outer, inner, p, s, z, y = place(pair_size, seq_size)
    f32, bf16 = jnp.float32, jnp.bfloat16
    rows_here = q_ref.shape[0]
    answer_rows, prefix_rows = a_in.shape[2], p_in.shape[2]
    total_rows = group * rows_here
    scaling = HEAD_DIM**-0.5
    first = s * rows_here
    others = range(1, pair_size)
    mates = range(1, inner)
    line = range(1, outer)
    for c in range(kv_heads):
        cut = slice(c * HEAD_DIM, (c + 1) * HEAD_DIM)
        p_in[c, 0] = pk_in[:, cut]
        p_in[c, 1] = pv_in[:, cut]
        for b in range(batch):
            at = b * kv_heads + c
            cut = slice(at * HEAD_DIM, (at + 1) * HEAD_DIM)
            a_in[c * batch + b, 0] = ak_in[:, cut]
            a_in[c * batch + b, 1] = av_in[:, cut]
    greet(pair_size, outer, inner, p, z, y)
    sends = []

    def send(src, dst, s_sem, r_sem, device):
        copy = pltpu.make_async_remote_copy(
            src_ref=src, dst_ref=dst, send_sem=s_sem, recv_sem=r_sem, device_id=device
        )
        copy.start()
        sends.append(copy)
        return copy

    def line_device(k):
        return {"seq": ((z + k) % outer) * inner + y}

    def mate_device(j):
        return {"seq": z * inner + (y + j) % inner}

    gpz, gaz, gpy, gay, gpx = {}, {}, {}, {}, {}

    def start_prefix(c):
        mine = p_g.at[c, p * seq_size + s]
        for k in line:
            gpz[c, k] = send(p_in.at[c], mine, gpz_s.at[c, k - 1], gpz_r.at[c, k - 1], line_device(k))
        prefix_to_mate(c, 0, p_in.at[c], s)
        prefix_to_side(c, 0, p_in.at[c], s)
        p_g[c, p * seq_size + s] = p_in[c]

    def prefix_to_mate(c, k, src, slot):
        for j in mates:
            at = (j - 1) * outer + k
            gpy[c, j, k] = send(
                src, p_g.at[c, p * seq_size + slot], gpy_s.at[c, at], gpy_r.at[c, at], mate_device(j)
            )

    def prefix_to_side(c, index, src, slot):
        for i in others:
            at = (i - 1) * seq_size + index
            gpx[c, i, index] = send(
                src,
                p_g.at[c, p * seq_size + slot],
                gpx_s.at[c, at],
                gpx_r.at[c, at],
                {"pair": (p + i) % pair_size},
            )

    def answer_to_mate(t, k, src, slot):
        for j in mates:
            at = (j - 1) * outer + k
            gay[t, j, k] = send(src, a_g.at[t, slot], gay_s.at[t, at], gay_r.at[t, at], mate_device(j))

    def start_answer(t):
        for k in line:
            gaz[t, k] = send(a_in.at[t], a_g.at[t, s], gaz_s.at[t, k - 1], gaz_r.at[t, k - 1], line_device(k))
        answer_to_mate(t, 0, a_in.at[t], s)
        a_g[t, s] = a_in[t]

    def pass_prefix_line(c):
        for k in line:
            slot = ((z + outer - k) % outer) * inner + y
            gpz[c, k].wait_recv()
            src = p_g.at[c, p * seq_size + slot]
            prefix_to_mate(c, k, src, slot)
            prefix_to_side(c, k, src, slot)

    def pass_answer_line(t):
        for k in line:
            slot = ((z + outer - k) % outer) * inner + y
            gaz[t, k].wait_recv()
            answer_to_mate(t, k, a_g.at[t, slot], slot)

    def pass_prefix_mate(c):
        for k in range(outer):
            for j in mates:
                slot = ((z + outer - k) % outer) * inner + (y + inner - j) % inner
                gpy[c, j, k].wait_recv()
                prefix_to_side(c, j * outer + k, p_g.at[c, p * seq_size + slot], slot)

    def ready_prefix(c):
        for i in others:
            for index in range(seq_size):
                gpx[c, i, index].wait_recv()

    def ready_answer(t):
        for k in range(outer):
            for j in mates:
                gay[t, j, k].wait_recv()

    order = list(line) + [0]
    spx, spy, spz, say, saz = {}, {}, {}, {}, {}

    def prefix_side(c, i):
        for j in list(mates) + [0]:
            for k in order:
                slot = ((z + k) % outer) * inner + (y + j) % inner
                at = (i - 1) * seq_size + j * outer + k
                spx[c, i, j, k] = send(
                    pt_ref.at[c, i - 1, slot],
                    rx.at[c, at],
                    spx_s.at[c, at],
                    spx_r.at[c, at],
                    {"pair": (p + i) % pair_size},
                )

    def side_sum(c, j, k):
        slot = ((z + k) % outer) * inner + (y + j) % inner
        total = pt_ref[c, pair_size - 1, slot].astype(f32)
        for i in others:
            spx[c, i, j, k].wait_recv()
            total += rx[c, (i - 1) * seq_size + j * outer + k].astype(f32)
        return total

    def prefix_mate(c):
        for k in order:
            for j in mates:
                at = (j - 1) * outer + k
                sy_p[c, at] = side_sum(c, j, k).astype(bf16)
                spy[c, j, k] = send(
                    sy_p.at[c, at], ry_p.at[c, at], spy_s.at[c, at], spy_r.at[c, at], mate_device(j)
                )

    def prefix_line(c):
        for k in order:
            total = side_sum(c, 0, k)
            for j in mates:
                spy[c, j, k].wait_recv()
                total += ry_p[c, (j - 1) * outer + k].astype(f32)
            if k > 0:
                sz_p[c, k - 1] = total.astype(bf16)
                spz[c, k] = send(
                    sz_p.at[c, k - 1], rz_p.at[c, k - 1], spz_s.at[c, k - 1], spz_r.at[c, k - 1], line_device(k)
                )
            else:
                own_p[c] = total

    def prefix_end(c):
        total = own_p[c]
        for k in line:
            spz[c, k].wait_recv()
            total += rz_p[c, k - 1].astype(f32)
        columns = slice(c * HEAD_DIM, (c + 1) * HEAD_DIM)
        pk_ref[:, columns] = total[0]
        pv_ref[:, columns] = total[1]

    def answer_mate(t):
        for k in order:
            for j in mates:
                at = (j - 1) * outer + k
                slot = ((z + k) % outer) * inner + (y + j) % inner
                say[t, j, k] = send(
                    at_ref.at[t, slot], ry_a.at[t, at], say_s.at[t, at], say_r.at[t, at], mate_device(j)
                )

    def answer_line(t):
        for k in order:
            slot = ((z + k) % outer) * inner + y
            total = at_ref[t, slot].astype(f32)
            for j in mates:
                say[t, j, k].wait_recv()
                total += ry_a[t, (j - 1) * outer + k].astype(f32)
            if k > 0:
                sz_a[t, k - 1] = total.astype(bf16)
                saz[t, k] = send(
                    sz_a.at[t, k - 1], rz_a.at[t, k - 1], saz_s.at[t, k - 1], saz_r.at[t, k - 1], line_device(k)
                )
            else:
                own_a[t] = total

    def answer_end(t, c, b):
        total = own_a[t]
        for k in line:
            saz[t, k].wait_recv()
            total += rz_a[t, k - 1].astype(f32)
        at = b * kv_heads + c
        columns = slice(at * HEAD_DIM, (at + 1) * HEAD_DIM)
        ak_ref[:, columns] = total[0].astype(bf16)
        av_ref[:, columns] = total[1].astype(bf16)

    lane = lax.broadcasted_iota(jnp.int32, (1, total_rows), 1)
    row = lax.broadcasted_iota(jnp.int32, (total_rows, 1), 0)
    lane_place = first + lax.rem(lane, rows_here)
    row_place = first + lax.rem(row, rows_here)

    def dot(left, right, a, b):
        return lax.dot_general(left, right, (((a,), (b,)), ((), ())), preferred_element_type=f32)

    def compute(t, c, b, between, last):
        limit, length = limits[0, b], lengths[0, b]
        heads = [(b * kv_heads + c) * group + g for g in range(group)]
        columns = [slice(h * HEAD_DIM, (h + 1) * HEAD_DIM) for h in heads]
        q = jnp.concatenate([q_ref[:, cut] for cut in columns], axis=0)
        d = jnp.concatenate([d_ref[:, cut] for cut in columns], axis=0)
        d = jnp.where(row_place < length, d.astype(f32), 0.0)
        d_t = d.T
        d = d.astype(bf16)
        work = []
        at = 0
        for i in range(pair_size):
            side = (p + 1 + i) % pair_size
            for low, high in chunks_of(seq_size, 8):
                span = (high - low) * prefix_rows
                work.append((i, low, high, side * seq_size + low, slice(at, at + span), span))
                at += span
        for low, high in chunks_of(seq_size, 4):
            span = (high - low) * answer_rows
            work.append((-1, low, high, low, slice(at, at + span), span))
            at += span

        def rows_of(i, low, high, begin, which):
            if i >= 0:
                return flat_rows(p_g[c, pl.ds(begin, high - low), which])
            return flat_rows(a_g[t, low:high, which])

        top = jnp.full((1, total_rows), FILL, f32)
        for i, low, high, begin, where, span in work:
            scores = dot(rows_of(i, low, high, begin, 0), q, 1, 1) * (scaling * math.log2(math.e))
            place_j = lax.broadcasted_iota(jnp.int32, (span, 1), 0)
            if i >= 0:
                allowed = begin * prefix_rows + place_j < limit
            else:
                allowed = begin * answer_rows + place_j <= lane_place
            scores = jnp.where(allowed, scores, FILL)
            top = jnp.maximum(top, jnp.max(scores, axis=0, keepdims=True))
            e_ref[where, :] = scores
        between(0)
        exp_total = jnp.zeros((1, total_rows), f32)
        for i, low, high, begin, where, span in work:
            e = jnp.exp2(e_ref[where, :] - top)
            exp_total = exp_total + jnp.sum(e, axis=0, keepdims=True)
            e_ref[where, :] = e
        inverse = 1.0 / exp_total
        between(1)
        attended = jnp.zeros((HEAD_DIM, total_rows), f32)
        for i, low, high, begin, where, span in work:
            probs = e_ref[where, :] * inverse
            probs_low = probs.astype(bf16)
            e_ref[where, :] = probs
            low_ref[where, :] = probs_low
            attended = attended + dot(rows_of(i, low, high, begin, 1), probs_low, 0, 0)
        attended = jnp.where(lane_place < length, attended, 0.0)
        delta = jnp.sum(d_t * attended, axis=0, keepdims=True)
        attended = attended.T.astype(bf16)
        for g, cut in enumerate(columns):
            out_ref[:, cut] = attended[g * rows_here : (g + 1) * rows_here]
        between(2)
        grad = jnp.zeros((HEAD_DIM, total_rows), f32)
        for i, low, high, begin, where, span in work:
            grad_probs = dot(rows_of(i, low, high, begin, 1), d, 1, 1)
            grad_low = (e_ref[where, :] * (grad_probs - delta)).astype(bf16)
            grad = grad + dot(rows_of(i, low, high, begin, 0), grad_low, 0, 0)
            key_term = dot(grad_low, q, 1, 0) * scaling
            value_term = dot(low_ref[where, :], d, 1, 0)
            for which, term in ((0, key_term), (1, value_term)):
                if i < 0:
                    at_ref[t, low:high, which] = term.astype(bf16).reshape(high - low, answer_rows, HEAD_DIM)
                    continue
                if b > 0:
                    term = acc_ref[which, where, :] + term
                if b < batch - 1:
                    acc_ref[which, where, :] = term
                else:
                    pt_ref[c, i, low:high, which] = term.astype(bf16).reshape(
                        high - low, prefix_rows, HEAD_DIM
                    )
            if b == batch - 1 and 0 <= i < pair_size - 1 and high == seq_size:
                prefix_side(c, i + 1)
        answer_mate(t)
        grad = (grad * scaling).T.astype(bf16)
        for g, cut in enumerate(columns):
            dq_ref[:, cut] = grad[g * rows_here : (g + 1) * rows_here]

    items = [(c, b) for c in range(kv_heads) for b in range(batch)]
    count = len(items)
    for t, (c, b) in enumerate(items):
        if b == 0:
            start_prefix(c)
        start_answer(t)

    def prepare(t):
        if t < count:
            if items[t][1] == 0:
                pass_prefix_line(items[t][0])
            pass_answer_line(t)

    def prepare_mate(t):
        if t < count and items[t][1] == 0:
            pass_prefix_mate(items[t][0])

    prepare(0)
    prepare_mate(0)
    prepare(1)
    for t, (c, b) in enumerate(items):
        if b == 0:
            ready_prefix(c)
        ready_answer(t)

        def between(stage, t=t, c=c, b=b):
            if stage == 0:
                prepare(t + 2)
            if stage == 1:
                if t > 0:
                    answer_line(t - 1)
                if b == 0 and c > 0:
                    prefix_mate(c - 1)
            if stage == 2:
                prepare_mate(t + 2)
                if b == 0 and c > 0:
                    prefix_line(c - 1)

        compute(t, c, b, between, t == count - 1)
    prefix_mate(kv_heads - 1)
    answer_line(count - 1)
    prefix_line(kv_heads - 1)
    for t, (c, b) in enumerate(items):
        answer_end(t, c, b)
    for c in range(kv_heads):
        prefix_end(c)
    for copy in sends:
        copy.wait_send()


def layer(pair_size, seq_size, batch, kv_heads, limits, lengths, q, d, ak, av, pk, pv):
    outer, inner = split_seq(seq_size)
    dma = pltpu.SemaphoreType.DMA
    low, f32 = jnp.bfloat16, jnp.float32
    rows_here, width = q.shape
    items = batch * kv_heads
    group = width // HEAD_DIM // items
    answer_rows, prefix_rows = ak.shape[0], pk.shape[0]
    a_one, p_one = (2, answer_rows, HEAD_DIM), (2, prefix_rows, HEAD_DIM)
    i1, o1, q1 = max(inner - 1, 1), max(outer - 1, 1), max(pair_size - 1, 1)
    prefix_keys = pair_size * seq_size * prefix_rows
    keys = prefix_keys + seq_size * answer_rows
    total_rows = group * rows_here
    semaphores = []
    for shape in 2 * (
        (items, o1), (kv_heads, o1), (items, i1 * outer), (kv_heads, i1 * outer), (kv_heads, q1 * seq_size)
    ):
        semaphores += [dma(shape), dma(shape)]
    answer_out = jax.ShapeDtypeStruct((answer_rows, items * HEAD_DIM), low)
    prefix_out = jax.ShapeDtypeStruct((prefix_rows, kv_heads * HEAD_DIM), f32)
    return pl.pallas_call(
        functools.partial(layer_kernel, pair_size, seq_size, batch, kv_heads, group),
        out_shape=(
            jax.ShapeDtypeStruct(q.shape, low),
            jax.ShapeDtypeStruct(q.shape, low),
            answer_out, answer_out, prefix_out, prefix_out,
        ),
        in_specs=[pl.BlockSpec(memory_space=pltpu.SMEM)] * 2 + [pl.BlockSpec(memory_space=VM)] * 6,
        out_specs=(pl.BlockSpec(memory_space=VM),) * 6,
        scratch_shapes=[
            VM((items,) + a_one, low),
            VM((kv_heads,) + p_one, low),
            VM((items, seq_size) + a_one, low),
            VM((kv_heads, pair_size * seq_size) + p_one, low),
            VM((items, seq_size) + a_one, low),
            VM((kv_heads, pair_size, seq_size) + p_one, low),
            VM((keys, total_rows), f32),
            VM((keys, total_rows), low),
            VM((2, prefix_keys, HEAD_DIM), f32),
            VM((kv_heads, q1 * seq_size) + p_one, low),
            VM((kv_heads, i1 * outer) + p_one, low),
            VM((kv_heads, o1) + p_one, low),
            VM((items, i1 * outer) + a_one, low),
            VM((items, o1) + a_one, low),
            VM((kv_heads, i1 * outer) + p_one, low),
            VM((kv_heads, o1) + p_one, low),
            VM((items, o1) + a_one, low),
            VM((items,) + a_one, f32),
            VM((kv_heads,) + p_one, f32),
        ] + semaphores,
        compiler_params=pltpu.CompilerParams(
            collective_id=0, has_side_effects=True, vmem_limit_bytes=60 * 1024 * 1024
        ),
        name="attention_layer",
    )(limits, lengths, q, d, ak, av, pk, pv)


def on_device(
    pair_size,
    seq_size,
    queries,
    answer_keys,
    answer_values,
    prefix_keys,
    prefix_values,
    grad_out,
    answer_length,
    prefix_limit,
):
    _, rows, batch, width = queries.shape
    size = HEAD_DIM
    kv_heads = answer_keys.shape[3] // size
    flat = (rows, batch * width)
    flat_keys = (rows, batch * kv_heads * size)
    out, dq, ak, av, pk, pv = layer(
        pair_size, seq_size, batch, kv_heads, prefix_limit, answer_length,
        queries.reshape(flat), grad_out.reshape(flat),
        answer_keys.reshape(flat_keys), answer_values.reshape(flat_keys), prefix_keys, prefix_values,
    )
    return (
        out.reshape(queries.shape),
        dq.reshape(queries.shape),
        ak.reshape(answer_keys.shape),
        av.reshape(answer_values.shape),
        pk,
        pv,
    )


def solution(mesh):
    rows = P("pair", "seq", None, "head")
    prefix = P(("pair", "seq"), "head")
    return jax.shard_map(
        functools.partial(on_device, mesh.shape["pair"], mesh.shape["seq"]),
        mesh=mesh,
        in_specs=(rows, rows, rows, prefix, prefix, rows, P("pair", None), P("pair", None)),
        out_specs=(rows, rows, rows, rows, prefix, prefix),
        check_vma=False,
    )
```

profile of v0, /device:TPU:0, one launch (start us, length us, event | category | flops | bytes accessed | tf_op | source)
XLA Modules:
  0.0 73.7 jit_solution(718797817812828054)
XLA Ops:
  0.6 0.0 copy-start.2
  0.6 1.5 %copy.16 = bf16[8,8,2,256]{3,1,2,0:T(8,128)(2,1)} copy(bf16[8,8,2,256]{3,2,1,0:T(2,128)(2,1)} %bitcast.18) | data formatting | bytes 131072
  2.2 0.0 copy-done.2
  2.2 0.6 copy.17
  2.8 0.0 copy-start
  2.8 1.9 %copy.14 = bf16[8,8,2,1792]{3,1,2,0:T(8,128)(2,1)} copy(bf16[8,8,2,1792]{3,2,1,0:T(2,128)(2,1)} %bitcast.14) | data formatting | bytes 917504
  4.7 0.0 copy-done
  4.7 0.8 %copy.15 = bf16[8,8,2,1792]{3,1,2,0:T(8,128)(2,1)} copy(bf16[8,8,2,1792]{3,2,1,0:T(2,128)(2,1)S(1)} %bitcast.15) | data formatting | bytes 917504
  5.5 62.5 %attention_layer.1 = (bf16[64,3584]{1,0:T(8,128)(2,1)}, bf16[64,3584]{1,0:T(8,128)(2,1)}, bf16[64,512]{1,0:T(8,128)(2,1)}, bf16[64,512]{1,0:T(8,128)(2,1)}, f32[48,256]{1,0:T(8,128)}, /*index=5*/f32[48,256]{1,0:T(8,128)}) custom-call(s32[1,2]{1,0:T(1,128)} %limits.1, s32[1,2]{1,0:T(1,128)} %lengths.1, bf16[64,3584]{1,0:T(8,128)(2,1)} %bitcast.12, ...), custom_call_target="tpu_custom_call" | custom-call | tf_op jit(solution)/shard_map/attention_layer/pallas_call | solution.py:417
  68.0 0.0 copy-start.4
  68.0 0.0 copy-start.1
  68.0 1.9 %reshape.40 = bf16[1,64,2,1792]{3,2,1,0:T(2,128)(2,1)} reshape(bf16[64,3584]{1,0:T(8,128)(2,1)} %get-tuple-element.12) | data formatting | bytes 917504 | tf_op jit(solution)/shard_map/reshape | solution.py:477
  69.9 0.0 copy-done.4
  69.9 0.0 copy-start.3
  69.9 0.6 reshape.42
  70.6 0.2 copy-done.3
  70.8 0.6 reshape.43
  71.4 0.0 copy-done.1
  71.4 0.0 copy-start.6
  71.4 0.9 %reshape.41 = bf16[1,64,2,1792]{3,2,1,0:T(2,128)(2,1)} reshape(bf16[64,3584]{1,0:T(8,128)(2,1)S(1)} %copy-done.1) | data formatting | bytes 917504 | tf_op jit(solution)/shard_map/reshape | solution.py:478
  72.3 0.0 copy-done.6
  72.3 0.0 copy-start.5
  72.3 0.6 copy.20
  72.9 0.2 copy-done.5
  73.1 0.6 copy.21
Async XLA Ops:
  0.6 1.5 %copy-start.2 = (bf16[1,64,2,256]{3,2,1,0:T(2,128)(2,1)S(1)}, bf16[1,64,2,256]{3,2,1,0:T(2,128)(2,1)}, u32[]{:S(2)}) copy-start(bf16[1,64,2,256]{3,2,1,0:T(2,128)(2,1)} %param.10) | copy-start | bytes 196612
  2.8 1.9 %copy-start = (bf16[1,64,2,1792]{3,2,1,0:T(2,128)(2,1)S(1)}, bf16[1,64,2,1792]{3,2,1,0:T(2,128)(2,1)}, u32[]{:S(2)}) copy-start(bf16[1,64,2,1792]{3,2,1,0:T(2,128)(2,1)} %param.13) | copy-start | bytes 1376260
  68.0 2.0 %copy-start.4 = (bf16[64,512]{1,0:T(8,128)(2,1)S(1)}, bf16[64,512]{1,0:T(8,128)(2,1)}, u32[]{:S(2)}) copy-start(bf16[64,512]{1,0:T(8,128)(2,1)} %get-tuple-element.14) | copy-start | bytes 196612
  68.0 3.4 %copy-start.1 = (bf16[64,3584]{1,0:T(8,128)(2,1)S(1)}, bf16[64,3584]{1,0:T(8,128)(2,1)}, u32[]{:S(2)}) copy-start(bf16[64,3584]{1,0:T(8,128)(2,1)} %get-tuple-element.13) | copy-start | bytes 1376260
  69.9 0.8 %copy-start.3 = (bf16[64,512]{1,0:T(8,128)(2,1)S(1)}, bf16[64,512]{1,0:T(8,128)(2,1)}, u32[]{:S(2)}) copy-start(bf16[64,512]{1,0:T(8,128)(2,1)} %get-tuple-element.15) | copy-start | bytes 196612
  71.4 0.9 %copy-start.6 = (f32[48,256]{1,0:T(8,128)S(1)}, f32[48,256]{1,0:T(8,128)}, u32[]{:S(2)}) copy-start(f32[48,256]{1,0:T(8,128)} %get-tuple-element.28) | copy-start | bytes 147460
  72.3 0.8 %copy-start.5 = (f32[48,256]{1,0:T(8,128)S(1)}, f32[48,256]{1,0:T(8,128)}, u32[]{:S(2)}) copy-start(f32[48,256]{1,0:T(8,128)} %get-tuple-element.29) | copy-start | bytes 147460
where the time goes:
time: 74.1 us; the launch traced here: 73.7 us
  Pallas kernels  62.5 us (84%)
  local copies, waits for them, and re-layouts  10.6 us (14%)
    pallas_call x1, Pallas kernels, layer(): pl.pallas_call(functools.partial(layer_kernel, pair_size, seq_size, batch...  62.5 us
    unnamed x20, local copies, waits for them, and re-layouts  6.49 us
    reshape x1, local copies, waits for them, and re-layouts, on_device(): out.reshape(queries.shape)  1.94 us

commit v1 on v0

--- a/solution.py
+++ b/solution.py
@@ -34,7 +34,17 @@
         pl.semaphore_signal(barrier, inc=1, device_id={"seq": z * inner + (y + j) % inner})
     for k in range(1, outer):
         pl.semaphore_signal(barrier, inc=1, device_id={"seq": ((z + k) % outer) * inner + y})
-    pl.semaphore_wait(barrier, pair_size + inner + outer - 3)
+
+
+def greeted(pair_size, outer, inner):
+    pl.semaphore_wait(pltpu.get_barrier_semaphore(), pair_size + inner + outer - 3)
+
+
+def only(when, act):
+    if when is None:
+        act()
+    else:
+        pl.when(when)(act)
 
 
 def chunks_of(slots, most):
@@ -51,13 +61,14 @@
     limits, lengths, q_ref, d_ref, ak_in, av_in, pk_in, pv_in,
     out_ref, dq_ref, ak_ref, av_ref, pk_ref, pv_ref,
     a_in, p_in, a_g, p_g, at_ref, pt_ref, e_ref, low_ref, acc_ref,
-    rx, ry_p, rz_p, ry_a, rz_a, sy_p, sz_p, sz_a, own_a, own_p,
+    rx, ry_p, rz_p, ry_a, rz_a, sy_p, sz_p, sz_a, own_a, own_p, q_s, d_s, o_s,
     gaz_s, gaz_r, gpz_s, gpz_r, gay_s, gay_r, gpy_s, gpy_r, gpx_s, gpx_r,
     saz_s, saz_r, spz_s, spz_r, say_s, say_r, spy_s, spy_r, spx_s, spx_r,
 ):
     outer, inner, p, s, z, y = place(pair_size, seq_size)
     f32, bf16 = jnp.float32, jnp.bfloat16
     rows_here = q_ref.shape[0]
+    pairs = rows_here * batch
     answer_rows, prefix_rows = a_in.shape[2], p_in.shape[2]
     total_rows = group * rows_here
     scaling = HEAD_DIM**-0.5
@@ -65,24 +76,51 @@
     others = range(1, pair_size)
     mates = range(1, inner)
     line = range(1, outer)
+
+    def shuffle(back):
+        new = lax.broadcasted_iota(jnp.int32, (pairs, pairs), 1 if back else 0)
+        old = lax.broadcasted_iota(jnp.int32, (pairs, pairs), 0 if back else 1)
+        return (lax.rem(new, rows_here) * batch + lax.div(new, rows_here) == old).astype(f32).astype(bf16)
+
+    def split_batch(block):
+        flat = jnp.dot(shuffle(False), block.reshape(pairs, HEAD_DIM), preferred_element_type=f32).astype(bf16)
+        return [flat[b * rows_here : (b + 1) * rows_here] for b in range(batch)]
+
+    def join_batch(parts):
+        flat = jnp.dot(shuffle(True), jnp.concatenate(parts, axis=0), preferred_element_type=f32).astype(bf16)
+        return flat.reshape(rows_here, batch, HEAD_DIM)
+
     for c in range(kv_heads):
         cut = slice(c * HEAD_DIM, (c + 1) * HEAD_DIM)
         p_in[c, 0] = pk_in[:, cut]
         p_in[c, 1] = pv_in[:, cut]
-        for b in range(batch):
-            at = b * kv_heads + c
-            cut = slice(at * HEAD_DIM, (at + 1) * HEAD_DIM)
-            a_in[c * batch + b, 0] = ak_in[:, cut]
-            a_in[c * batch + b, 1] = av_in[:, cut]
+        for which, source in enumerate((ak_in, av_in)):
+            for b, part in enumerate(split_batch(source[:, :, cut])):
+                a_in[c * batch + b, which] = part
+    for slot in range(1, seq_size):
+
+        def clear(slot=slot):
+            a_g[:, slot] = jnp.zeros((a_g.shape[0],) + a_g.shape[2:], bf16)
+
+        only(s < slot, clear)
     greet(pair_size, outer, inner, p, z, y)
+    for c in range(kv_heads):
+        for g in range(group):
+            cut = slice((c * group + g) * HEAD_DIM, (c * group + g + 1) * HEAD_DIM)
+            rows = slice(g * rows_here, (g + 1) * rows_here)
+            for b, part in enumerate(split_batch(q_ref[:, :, cut])):
+                q_s[c * batch + b, rows] = part
+            for b, part in enumerate(split_batch(d_ref[:, :, cut])):
+                d_s[c * batch + b, rows] = part
+    greeted(pair_size, outer, inner)
     sends = []
 
-    def send(src, dst, s_sem, r_sem, device):
+    def send(src, dst, s_sem, r_sem, device, when=None):
         copy = pltpu.make_async_remote_copy(
             src_ref=src, dst_ref=dst, send_sem=s_sem, recv_sem=r_sem, device_id=device
         )
-        copy.start()
-        sends.append(copy)
+        only(when, copy.start)
+        sends.append((when, copy))
         return copy
 
     def line_device(k):
@@ -122,11 +160,14 @@
     def answer_to_mate(t, k, src, slot):
         for j in mates:
             at = (j - 1) * outer + k
-            gay[t, j, k] = send(src, a_g.at[t, slot], gay_s.at[t, at], gay_r.at[t, at], mate_device(j))
+            when = z >= k if k > 0 else y + j < inner
+            gay[t, j, k] = send(src, a_g.at[t, slot], gay_s.at[t, at], gay_r.at[t, at], mate_device(j), when)
 
     def start_answer(t):
         for k in line:
-            gaz[t, k] = send(a_in.at[t], a_g.at[t, s], gaz_s.at[t, k - 1], gaz_r.at[t, k - 1], line_device(k))
+            gaz[t, k] = send(
+                a_in.at[t], a_g.at[t, s], gaz_s.at[t, k - 1], gaz_r.at[t, k - 1], line_device(k), z + k < outer
+            )
         answer_to_mate(t, 0, a_in.at[t], s)
         a_g[t, s] = a_in[t]
 
@@ -141,7 +182,7 @@
     def pass_answer_line(t):
         for k in line:
             slot = ((z + outer - k) % outer) * inner + y
-            gaz[t, k].wait_recv()
+            only(z >= k, gaz[t, k].wait_recv)
             answer_to_mate(t, k, a_g.at[t, slot], slot)
 
     def pass_prefix_mate(c):
@@ -159,7 +200,7 @@
     def ready_answer(t):
         for k in range(outer):
             for j in mates:
-                gay[t, j, k].wait_recv()
+                only(z >= k if k > 0 else y >= j, gay[t, j, k].wait_recv)
 
     order = list(line) + [0]
     spx, spy, spz, say, saz = {}, {}, {}, {}, {}
@@ -223,33 +264,47 @@
                 at = (j - 1) * outer + k
                 slot = ((z + k) % outer) * inner + (y + j) % inner
                 say[t, j, k] = send(
-                    at_ref.at[t, slot], ry_a.at[t, at], say_s.at[t, at], say_r.at[t, at], mate_device(j)
+                    at_ref.at[t, slot], ry_a.at[t, at], say_s.at[t, at], say_r.at[t, at], mate_device(j),
+                    z + k >= outer if k > 0 else y + j >= inner,
                 )
 
     def answer_line(t):
-        for k in order:
-            slot = ((z + k) % outer) * inner + y
-            total = at_ref[t, slot].astype(f32)
-            for j in mates:
-                say[t, j, k].wait_recv()
-                total += ry_a[t, (j - 1) * outer + k].astype(f32)
-            if k > 0:
+        for k in line:
+
+            def pass_down(k=k):
+                total = at_ref[t, (z + k - outer) * inner + y].astype(f32)
+                for j in mates:
+                    say[t, j, k].wait_recv()
+                    total += ry_a[t, (j - 1) * outer + k].astype(f32)
                 sz_a[t, k - 1] = total.astype(bf16)
-                saz[t, k] = send(
-                    sz_a.at[t, k - 1], rz_a.at[t, k - 1], saz_s.at[t, k - 1], saz_r.at[t, k - 1], line_device(k)
-                )
-            else:
-                own_a[t] = total
+
+            only(z + k >= outer, pass_down)
+            saz[t, k] = send(
+                sz_a.at[t, k - 1], rz_a.at[t, k - 1], saz_s.at[t, k - 1], saz_r.at[t, k - 1], line_device(k),
+                z + k >= outer,
+            )
+        own_a[t] = at_ref[t, s].astype(f32)
+        for j in mates:
+
+            def add_mate(j=j):
+                say[t, j, 0].wait_recv()
+                own_a[t] += ry_a[t, (j - 1) * outer].astype(f32)
+
+            only(y < j, add_mate)
 
     def answer_end(t, c, b):
-        total = own_a[t]
-        for k in line:
-            saz[t, k].wait_recv()
-            total += rz_a[t, k - 1].astype(f32)
-        at = b * kv_heads + c
-        columns = slice(at * HEAD_DIM, (at + 1) * HEAD_DIM)
-        ak_ref[:, columns] = total[0].astype(bf16)
-        av_ref[:, columns] = total[1].astype(bf16)
+        for k in line:
+
+            def add_line(k=k):
+                saz[t, k].wait_recv()
+                own_a[t] += rz_a[t, k - 1].astype(f32)
+
+            only(z < k, add_line)
+        if b < batch - 1:
+            return
+        columns = slice(c * HEAD_DIM, (c + 1) * HEAD_DIM)
+        for which, ref in enumerate((ak_ref, av_ref)):
+            ref[:, :, columns] = join_batch([own_a[c * batch + i, which].astype(bf16) for i in range(batch)])
 
     lane = lax.broadcasted_iota(jnp.int32, (1, total_rows), 1)
     row = lax.broadcasted_iota(jnp.int32, (total_rows, 1), 0)
@@ -261,10 +316,7 @@
 
     def compute(t, c, b, between, last):
         limit, length = limits[0, b], lengths[0, b]
-        heads = [(b * kv_heads + c) * group + g for g in range(group)]
-        columns = [slice(h * HEAD_DIM, (h + 1) * HEAD_DIM) for h in heads]
-        q = jnp.concatenate([q_ref[:, cut] for cut in columns], axis=0)
-        d = jnp.concatenate([d_ref[:, cut] for cut in columns], axis=0)
+        q, d = q_s[t], d_s[t]
         d = jnp.where(row_place < length, d.astype(f32), 0.0)
         d_t = d.T
         d = d.astype(bf16)
@@ -314,9 +366,7 @@
             attended = attended + dot(rows_of(i, low, high, begin, 1), probs_low, 0, 0)
         attended = jnp.where(lane_place < length, attended, 0.0)
         delta = jnp.sum(d_t * attended, axis=0, keepdims=True)
-        attended = attended.T.astype(bf16)
-        for g, cut in enumerate(columns):
-            out_ref[:, cut] = attended[g * rows_here : (g + 1) * rows_here]
+        o_s[0, b] = attended.T.astype(bf16)
         between(2)
         grad = jnp.zeros((HEAD_DIM, total_rows), f32)
         for i, low, high, begin, where, span in work:
@@ -340,9 +390,14 @@
             if b == batch - 1 and 0 <= i < pair_size - 1 and high == seq_size:
                 prefix_side(c, i + 1)
         answer_mate(t)
-        grad = (grad * scaling).T.astype(bf16)
-        for g, cut in enumerate(columns):
-            dq_ref[:, cut] = grad[g * rows_here : (g + 1) * rows_here]
+        o_s[1, b] = (grad * scaling).T.astype(bf16)
+        if b < batch - 1:
+            return
+        for which, ref in enumerate((out_ref, dq_ref)):
+            for g in range(group):
+                cut = slice((c * group + g) * HEAD_DIM, (c * group + g + 1) * HEAD_DIM)
+                rows = slice(g * rows_here, (g + 1) * rows_here)
+                ref[:, :, cut] = join_batch([o_s[which, i, rows] for i in range(batch)])
 
     items = [(c, b) for c in range(kv_heads) for b in range(batch)]
     count = len(items)
@@ -390,17 +445,17 @@
         answer_end(t, c, b)
     for c in range(kv_heads):
         prefix_end(c)
-    for copy in sends:
-        copy.wait_send()
+    for when, copy in sends:
+        only(when, copy.wait_send)
 
 
 def layer(pair_size, seq_size, batch, kv_heads, limits, lengths, q, d, ak, av, pk, pv):
     outer, inner = split_seq(seq_size)
     dma = pltpu.SemaphoreType.DMA
     low, f32 = jnp.bfloat16, jnp.float32
-    rows_here, width = q.shape
+    rows_here, _, width = q.shape
     items = batch * kv_heads
-    group = width // HEAD_DIM // items
+    group = width // HEAD_DIM // kv_heads
     answer_rows, prefix_rows = ak.shape[0], pk.shape[0]
     a_one, p_one = (2, answer_rows, HEAD_DIM), (2, prefix_rows, HEAD_DIM)
     i1, o1, q1 = max(inner - 1, 1), max(outer - 1, 1), max(pair_size - 1, 1)
@@ -412,7 +467,7 @@
         (items, o1), (kv_heads, o1), (items, i1 * outer), (kv_heads, i1 * outer), (kv_heads, q1 * seq_size)
     ):
         semaphores += [dma(shape), dma(shape)]
-    answer_out = jax.ShapeDtypeStruct((answer_rows, items * HEAD_DIM), low)
+    answer_out = jax.ShapeDtypeStruct(ak.shape, low)
     prefix_out = jax.ShapeDtypeStruct((prefix_rows, kv_heads * HEAD_DIM), f32)
     return pl.pallas_call(
         functools.partial(layer_kernel, pair_size, seq_size, batch, kv_heads, group),
@@ -443,12 +498,32 @@
             VM((items, o1) + a_one, low),
             VM((items,) + a_one, f32),
             VM((kv_heads,) + p_one, f32),
+            VM((items, total_rows, HEAD_DIM), low),
+            VM((items, total_rows, HEAD_DIM), low),
+            VM((2, batch, total_rows, HEAD_DIM), low),
         ] + semaphores,
         compiler_params=pltpu.CompilerParams(
             collective_id=0, has_side_effects=True, vmem_limit_bytes=60 * 1024 * 1024
         ),
         name="attention_layer",
     )(limits, lengths, q, d, ak, av, pk, pv)
+
+
+def hand_on(*refs):
+    half = len(refs) // 2
+    for source, target in zip(refs[:half], refs[half:]):
+        target[...] = source[...]
+
+
+def write_out(results):
+    return pl.pallas_call(
+        hand_on,
+        out_shape=tuple(jax.ShapeDtypeStruct(r.shape, r.dtype) for r in results),
+        in_specs=[pl.BlockSpec(memory_space=VM)] * len(results),
+        out_specs=(pl.BlockSpec(memory_space=VM),) * len(results),
+        compiler_params=pltpu.CompilerParams(vmem_limit_bytes=60 * 1024 * 1024),
+        name="write_out",
+    )(*results)
 
 
 def on_device(
@@ -466,13 +541,13 @@
     _, rows, batch, width = queries.shape
     size = HEAD_DIM
     kv_heads = answer_keys.shape[3] // size
-    flat = (rows, batch * width)
-    flat_keys = (rows, batch * kv_heads * size)
-    out, dq, ak, av, pk, pv = layer(
+    flat = queries.shape[1:]
+    flat_keys = answer_keys.shape[1:]
+    out, dq, ak, av, pk, pv = write_out(layer(
         pair_size, seq_size, batch, kv_heads, prefix_limit, answer_length,
         queries.reshape(flat), grad_out.reshape(flat),
         answer_keys.reshape(flat_keys), answer_values.reshape(flat_keys), prefix_keys, prefix_values,
-    )
+    ))
     return (
         out.reshape(queries.shape),
         dq.reshape(queries.shape),

time: 74.1 us -> 65 us (0.88)
  local copies, waits for them, and re-layouts: 10.6 us -> 0 us
  Pallas kernels: 62.5 us -> 64.2 us
    unnamed x20 -> x0, local copies, waits for them, and re-layouts: 6.49 us -> none
    reshape x4 -> x0, local copies, waits for them, and re-layouts: 4.11 us -> none  [the longest x1 1.94 us: on_device(): out.reshape(queries.shape)]
    pallas_call x0 -> x1, Pallas kernels: none -> 2.22 us  [write_out(): pl.pallas_call(hand_on, out_shape=tuple((jax.ShapeDtypeStruct(r.shape, r....]
where the time goes in v1:
time: 65 us; the launch traced here: 64.8 us
  Pallas kernels  64.2 us (99%)
    pallas_call x1, Pallas kernels, layer(): pl.pallas_call(functools.partial(layer_kernel, pair_size, seq_size, batch...  61.9 us
    pallas_call x1, Pallas kernels, write_out(): pl.pallas_call(hand_on, out_shape=tuple((jax.ShapeDtypeStruct(r.shape, r....  2.22 us

profile of v1, /device:TPU:0, one launch (start us, length us, event | category | flops | bytes accessed | tf_op | source)
XLA Modules:
  0.0 64.8 jit_solution(6780853254644363692)
XLA Ops:
  0.6 61.9 %attention_layer.1 = (bf16[64,2,1792]{2,1,0:T(2,128)(2,1)}, bf16[64,2,1792]{2,1,0:T(2,128)(2,1)}, bf16[64,2,256]{2,1,0:T(2,128)(2,1)}, bf16[64,2,256]{2,1,0:T(2,...) custom-call(s32[1,2]{1,0:T(1,128)} %limits.1, s32[1,2]{1,0:T(1,128)} %lengths.1, bf16[64,2,1792]{2,1,0:T(2,128)(2,1)} %bitcast.8, ...), custom_call_target="tpu_custom_call" | custom-call | tf_op jit(solution)/shard_map/attention_layer/pallas_call | solution.py:472
  62.6 2.2 %write_out.1 = (bf16[64,2,1792]{2,1,0:T(2,128)(2,1)}, bf16[64,2,1792]{2,1,0:T(2,128)(2,1)}, bf16[64,2,256]{2,1,0:T(2,128)(2,1)}, bf16[64,2,256]{2,1,0:T(2,128)(2...) custom-call(bf16[64,2,1792]{2,1,0:T(2,128)(2,1)} %get-tuple-element.18.refs_0_, ...), custom_call_target="tpu_custom_call" | custom-call | tf_op jit(solution)/shard_map/write_out/pallas_call | solution.py:519
